TPU v7x, 32 devices: a whole 2x2x4 slice. The times are simulated.
32 devices in a mesh: slab: 8 (over z, x), sub: 4 (over y, core).
Axes of the slice: x: 2, y: 2, z: 4, core: 2. Of those that a mesh axis runs over, the one named last changes fastest.
Arguments:
- values: float32 [768, 2, 128, 256], P(('slab', 'sub')), may hold values from -0.25 to 0.25
- block_ids: int32 [768, 2], P(('slab', 'sub')), may hold values from 0 to 383, as said below
- tile_counts: int32 [8, 4], P('slab', 'sub'), may hold values from 8 to 24, as said below
- right_side: float32 [768, 128], P(('slab', 'sub')), may hold values from -18 to 18
Outputs:
- solution: float32 [384, 256], P(('slab', 'sub'))
- residual: float32 [768, 128], P(('slab', 'sub'))
Inputs may be any that keep to these rules, and one draw needn't show every extreme that they name: `block_ids`: every block id names a node block held by a device of the row tile's own slab or of a slab one index of slab away; the first coupled block of each tile lies in its own slab. Block b is held by device b div 12. `tile_counts`: some device has all 24 slots live in every draw.
All inputs are finite; a program needn't handle non-finite values.
Results may differ from a plain program's by a relative error of at most 0.0003.
Values sent between devices are 32-bit elements; how exact they have to be, the bound alone decides.
A program may use at most 64 MiB of HBM per device.

v0:
```python
import jax
import jax.numpy as jnp
from jax import lax
from jax.sharding import PartitionSpec as P

ITERS = 4
NB_DEV = 12


precise = lax.Precision.HIGHEST


def with_halo(block, sides, width):
    for axis, dim in sides:
        count = lax.axis_size(axis)
        forward = [(i, i + 1) for i in range(count - 1)]
        backward = [(target, source) for source, target in forward]
        low = lax.ppermute(
            lax.slice_in_dim(block, block.shape[dim] - width, None, axis=dim), axis, forward
        )
        high = lax.ppermute(lax.slice_in_dim(block, 0, width, axis=dim), axis, backward)
        block = jnp.concatenate([low, block, high], axis=dim)
    return block


def from_behind(block, axis, distance):
    devices = range(lax.axis_size(axis))
    route = [(i - distance, i) for i in devices if i - distance in devices]
    return lax.ppermute(block, axis, route)


def per_device(values, block_ids, tile_counts, right_side):
    tiles_dev = values.shape[0]
    coupled = values.shape[1]
    block_len = values.shape[3]
    sub_count = lax.axis_size("sub")
    slab_index = lax.axis_index("slab")
    owner_dev = block_ids // NB_DEV
    rel_slab = owner_dev // sub_count - slab_index + 1
    window_ids = (rel_slab * sub_count + owner_dev % sub_count) * NB_DEV + block_ids % NB_DEV
    window_len = 3 * sub_count * NB_DEV
    selector = (
        window_ids.reshape(-1)[:, None] == jnp.arange(window_len, dtype=jnp.int32)[None, :]
    ).astype(jnp.float32)
    live_tiles = (jnp.arange(tiles_dev, dtype=jnp.int32) < tile_counts[0, 0]).astype(jnp.float32)

    def gather_window(field):
        gathered = lax.all_gather(field, "sub", axis=0, tiled=True)
        return with_halo(gathered, (("slab", 0),), sub_count * NB_DEV)

    def return_window(contrib):
        pieces = contrib.reshape(3, sub_count * NB_DEV, block_len)
        from_above = from_behind(pieces[0], "slab", -1)
        from_below = from_behind(pieces[2], "slab", 1)
        return lax.psum_scatter(
            pieces[1] + from_above + from_below, "sub", scatter_dimension=0, tiled=True
        )

    def forward(field):
        window = gather_window(field)
        picked = jnp.dot(selector, window, precision=precise).reshape(tiles_dev, coupled, block_len)
        image = jnp.einsum("tkij,tkj->ti", values, picked, precision=precise)
        return image * live_tiles[:, None]

    def spread_back(terms):
        flat_terms = terms.reshape(tiles_dev * coupled, block_len)
        return return_window(jnp.dot(selector.T, flat_terms, precision=precise))

    def backward(rows):
        return spread_back(jnp.einsum("tkij,ti->tkj", values, rows, precision=precise))

    squares = (
        jnp.einsum("tkij,tkij->tkj", values, values, precision=precise) * live_tiles[:, None, None]
    )
    jacobi = 1.0 / (1.0 + spread_back(squares))
    solution = jnp.zeros((NB_DEV, block_len), jnp.float32)
    residual = right_side * live_tiles[:, None]
    normal_res = backward(residual)
    scaled = jacobi * normal_res
    direction = scaled
    rho_now = lax.psum(jnp.sum(normal_res * scaled), ("slab", "sub"))
    for iteration in range(ITERS):
        image = forward(direction)
        back_image = backward(image)
        image_norm, cross_term, back_norm = lax.psum(
            (
                jnp.sum(image * image),
                jnp.sum(scaled * back_image),
                jnp.sum(back_image * jacobi * back_image),
            ),
            ("slab", "sub"),
        )
        step_size = rho_now / image_norm
        solution = solution + step_size * direction
        residual = residual - step_size * image
        normal_res = normal_res - step_size * back_image
        scaled = jacobi * normal_res
        rho_next = rho_now - 2.0 * step_size * cross_term + step_size * step_size * back_norm
        direction = scaled + rho_next / rho_now * direction
        rho_now = rho_next
    return (solution, residual)


def solution(mesh):
    in_specs = (
        P(("slab", "sub"), None, None, None),
        P(("slab", "sub"), None),
        P("slab", "sub"),
        P(("slab", "sub"), None),
    )
    out_specs = (P(("slab", "sub"), None), P(("slab", "sub"), None))
    return jax.shard_map(
        per_device, mesh=mesh, in_specs=in_specs, out_specs=out_specs, check_vma=False
    )
```

profile of v0, /device:TPU:0, one launch (start us, length us, event | category | flops | bytes accessed | tf_op | source)
XLA Modules:
  0.0 391.7 jit_solution(12818185539324030647)
XLA Ops:
  1.3 0.7 fusion.57
  2.2 0.8 broadcast_multiply_fusion.4
  3.0 5.1 %fusion.71 = f32[24,1,2,256]{3,1,2,0:T(1,128)S(1)} fusion(f32[24,128,1,1]{1,2,3,0:T(1,128)S(1)} %bitcast.94, f32[24,2,128,256]{3,2,1,0:T(8,128)} %param.4), kind=kOutput, calls=%fused_computation.110 | convolution fusion | flops 18874368 | bytes 6352896 | tf_op jit(solution)/shard_map/tkij,ti->tkj/dot_general | solution.py:70
  8.5 1.3 collective-permute-start
  9.8 5.5 %collective-permute-start.1 = (f32[48,256]{1,0:T(8,128)S(1)}, f32[48,256]{1,0:T(8,128)S(1)}, u32[]{:S(2)}, u32[]{:S(2)}) collective-permute-start(f32[48,256]{1,0:T(8,128)S(1)} %get-tuple-element.43), channel_id=1, source_target_pairs={{0,4},{4,8},{8,12},{12,16},{16,20},{20,24},{24,28},{1,5},{5,9},{9,... | collective-permute-start | bytes 147464 | tf_op jit(solution)/shard_map/ppermute | solution.py:29
  15.3 3.6 multiply_reduce_fusion
  19.4 1.3 collective-permute-start.2
  20.7 5.4 %collective-permute-start.3 = (f32[48,256]{1,0:T(8,128)S(1)}, f32[48,256]{1,0:T(8,128)S(1)}, u32[]{:S(2)}, u32[]{:S(2)}) collective-permute-start(f32[48,256]{1,0:T(8,128)S(1)} %get-tuple-element.41), channel_id=1, source_target_pairs={{0,4},{4,8},{8,12},{12,16},{16,20},{20,24},{24,28},{1,5},{5,9},{9,... | collective-permute-start | bytes 147464 | tf_op jit(solution)/shard_map/ppermute | solution.py:29
  26.3 1.6 collective-permute-done.3
  27.9 6.8 %fusion.63 = (f32[16,256]{1,0:T(8,128)S(1)}, f32[16,256]{1,0:T(8,128)S(1)}) fusion(f32[48,256]{1,0:T(8,128)S(1)} %fusion.33, f32[48,256]{1,0:T(8,128)S(1)} %fusion.32), kind=kCustom, calls=%all-reduce-scatter.5 | all-reduce-scatter fusion | flops 32769 | bytes 131584
  34.7 1.6 collective-permute-start.19
  36.2 4.2 %collective-permute-start.18 = (f32[12,256]{1,0:T(8,128)S(1)}, f32[12,256]{1,0:T(8,128)S(1)}, u32[]{:S(2)}, u32[]{:S(2)}) collective-permute-start(f32[12,256]{1,0:T(8,128)S(1)} %slice.90), channel_id=1, source_target_pairs={{0,1},{1,2},{2,3},{4,5},{5,6},{6,7},{8,9},{9,10},{10,11},{12,13},{... | collective-permute-start | bytes 36872
  42.0 5.2 %all-gather = f32[4,12,256]{2,1,0:T(8,128)S(1)} all-gather(f32[1,12,256]{2,1,0:T(8,128)S(1)} %bitcast.80), channel_id=1, replica_groups=mesh['slab'=8,'sub'=4] {'sub'}, dimensions={0}, use_global_device_ids=true | all-gather | bytes 61440 | tf_op jit(solution)/shard_map/all_gather | solution.py:48
  47.2 1.3 collective-permute-start.5
  48.5 5.4 %collective-permute-start.4 = (f32[48,256]{1,0:T(8,128)S(1)}, f32[48,256]{1,0:T(8,128)S(1)}, u32[]{:S(2)}, u32[]{:S(2)}) collective-permute-start(f32[48,256]{1,0:T(8,128)S(1)} %reshape.87), channel_id=1, source_target_pairs={{0,4},{4,8},{8,12},{12,16},{16,20},{20,24},{24,28},{1,5},{5,9},{9,... | collective-permute-start | bytes 147464 | tf_op jit(solution)/shard_map/ppermute | solution.py:18
  54.3 1.8 collective-permute-done.4
  56.4 7.3 %fusion.72 = f32[24,1,128,1]{2,1,3,0:T(1,128)S(1)} fusion(f32[24,2,256,1]{2,3,1,0:T(1,128)S(1)} %reshape.113, f32[24,2,128,256]{3,2,1,0:T(8,128)} %param.4), kind=kOutput, calls=%fused_computation.111 | convolution fusion | flops 18874368 | bytes 6352896 | tf_op jit(solution)/shard_map/tkij,tkj->ti/dot_general | solution.py:62
  63.7 0.7 multiply_reduce_fusion.8
  64.3 5.1 %fusion.73 = f32[24,1,2,256]{3,1,2,0:T(1,128)S(1)} fusion(f32[24,128,1,1]{1,2,3,0:T(1,128)S(1)} %bitcast.86, f32[24,2,128,256]{3,2,1,0:T(8,128)} %param.4), kind=kOutput, calls=%fused_computation.112 | convolution fusion | flops 18874368 | bytes 6352896 | tf_op jit(solution)/shard_map/tkij,ti->tkj/dot_general | solution.py:70
  69.9 1.3 collective-permute-start.6
  71.2 5.4 %collective-permute-start.7 = (f32[48,256]{1,0:T(8,128)S(1)}, f32[48,256]{1,0:T(8,128)S(1)}, u32[]{:S(2)}, u32[]{:S(2)}) collective-permute-start(f32[48,256]{1,0:T(8,128)S(1)} %get-tuple-element.39), channel_id=1, source_target_pairs={{0,4},{4,8},{8,12},{12,16},{16,20},{20,24},{24,28},{1,5},{5,9},{9,... | collective-permute-start | bytes 147464 | tf_op jit(solution)/shard_map/ppermute | solution.py:29
  76.6 1.6 collective-permute-done.7
  78.3 7.8 %fusion.2 = f32[16,256]{1,0:T(8,128)S(1)} fusion(f32[48,256]{1,0:T(8,128)S(1)} %fusion.31), kind=kCustom, calls=%all-reduce-scatter.2 | all-reduce-scatter fusion | flops 16385 | bytes 66048
  86.0 1.3 collective-permute-start.20
  87.3 0.8 collective-permute-done.20
  88.2 0.7 fusion.48
  88.9 45.8 %all-reduce.12 = (f32[]{:T(128)}, f32[]{:T(128)}, f32[]{:T(128)}, f32[]{:T(128)}) all-reduce(f32[]{:T(128)} %get-tuple-element.8, f32[]{:T(128)} %get-tuple-element.32, f32[]{:T(128)} %get-tuple-element.7, f32[]{:T(128)} %get-tuple-element.6), channel_id=1, replica_groups=mesh['slab'=8,'sub'=4] {'slab','sub'}, use_global_device_ids=true, to_apply=%region_3.4 | all-reduce | flops 4 | bytes 32 | tf_op jit(solution)/shard_map/psum | solution.py:81
  138.7 5.7 %all-gather.1 = f32[4,12,256]{2,1,0:T(8,128)S(1)} all-gather(f32[1,12,256]{2,1,0:T(8,128)S(1)} %get-tuple-element.29), channel_id=1, replica_groups=mesh['slab'=8,'sub'=4] {'sub'}, dimensions={0}, use_global_device_ids=true | all-gather | bytes 61440 | tf_op jit(solution)/shard_map/all_gather | solution.py:48
  144.5 1.3 collective-permute-start.9
  145.8 4.7 %collective-permute-start.8 = (f32[48,256]{1,0:T(8,128)S(1)}, f32[48,256]{1,0:T(8,128)S(1)}, u32[]{:S(2)}, u32[]{:S(2)}) collective-permute-start(f32[48,256]{1,0:T(8,128)S(1)} %reshape.89), channel_id=1, source_target_pairs={{0,4},{4,8},{8,12},{12,16},{16,20},{20,24},{24,28},{1,5},{5,9},{9,... | collective-permute-start | bytes 147464 | tf_op jit(solution)/shard_map/ppermute | solution.py:18
  150.5 1.5 collective-permute-done.8
  152.3 7.3 %fusion.74 = f32[24,1,128,1]{2,1,3,0:T(1,128)S(1)} fusion(f32[24,2,256,1]{2,3,1,0:T(1,128)S(1)} %reshape.115, f32[24,2,128,256]{3,2,1,0:T(8,128)} %param.4), kind=kOutput, calls=%fused_computation.113 | convolution fusion | flops 18874368 | bytes 6352896 | tf_op jit(solution)/shard_map/tkij,tkj->ti/dot_general | solution.py:62
  159.6 0.7 multiply_reduce_fusion.7
  160.3 5.1 %fusion.75 = f32[24,1,2,256]{3,1,2,0:T(1,128)S(1)} fusion(f32[24,128,1,1]{1,2,3,0:T(1,128)S(1)} %bitcast.87, f32[24,2,128,256]{3,2,1,0:T(8,128)} %param.4), kind=kOutput, calls=%fused_computation.114 | convolution fusion | flops 18874368 | bytes 6352896 | tf_op jit(solution)/shard_map/tkij,ti->tkj/dot_general | solution.py:70
  165.8 1.3 collective-permute-start.10
  167.1 5.3 %collective-permute-start.11 = (f32[48,256]{1,0:T(8,128)S(1)}, f32[48,256]{1,0:T(8,128)S(1)}, u32[]{:S(2)}, u32[]{:S(2)}) collective-permute-start(f32[48,256]{1,0:T(8,128)S(1)} %get-tuple-element.37), channel_id=1, source_target_pairs={{0,4},{4,8},{8,12},{12,16},{16,20},{20,24},{24,28},{1,5},{5,9},{9,... | collective-permute-start | bytes 147464 | tf_op jit(solution)/shard_map/ppermute | solution.py:29
  172.5 1.6 collective-permute-done.11
  174.1 7.8 %fusion.3 = f32[16,256]{1,0:T(8,128)S(1)} fusion(f32[48,256]{1,0:T(8,128)S(1)} %fusion.30), kind=kCustom, calls=%all-reduce-scatter.3 | all-reduce-scatter fusion | flops 16385 | bytes 66048
  182.0 1.3 collective-permute-start.21
  183.3 0.8 collective-permute-done.21
  184.2 0.7 fusion.49
  184.9 45.5 %all-reduce.11 = (f32[]{:T(128)}, f32[]{:T(128)}, f32[]{:T(128)}) all-reduce(f32[]{:T(128)} %get-tuple-element.27, f32[]{:T(128)} %get-tuple-element.5, f32[]{:T(128)} %get-tuple-element.4), channel_id=1, replica_groups=mesh['slab'=8,'sub'=4] {'slab','sub'}, use_global_device_ids=true, to_apply=%region_12.13 | all-reduce | flops 3 | bytes 24 | tf_op jit(solution)/shard_map/psum | solution.py:85
  232.4 5.7 %all-gather.2 = f32[4,12,256]{2,1,0:T(8,128)S(1)} all-gather(f32[1,12,256]{2,1,0:T(8,128)S(1)} %get-tuple-element.25), channel_id=1, replica_groups=mesh['slab'=8,'sub'=4] {'sub'}, dimensions={0}, use_global_device_ids=true | all-gather | bytes 61440 | tf_op jit(solution)/shard_map/all_gather | solution.py:48
  238.1 1.3 collective-permute-start.13
  239.4 4.5 %collective-permute-start.12 = (f32[48,256]{1,0:T(8,128)S(1)}, f32[48,256]{1,0:T(8,128)S(1)}, u32[]{:S(2)}, u32[]{:S(2)}) collective-permute-start(f32[48,256]{1,0:T(8,128)S(1)} %reshape.91), channel_id=1, source_target_pairs={{0,4},{4,8},{8,12},{12,16},{16,20},{20,24},{24,28},{1,5},{5,9},{9,... | collective-permute-start | bytes 147464 | tf_op jit(solution)/shard_map/ppermute | solution.py:18
  244.1 1.6 collective-permute-done.12
  245.9 7.3 %fusion.76 = f32[24,1,128,1]{2,1,3,0:T(1,128)S(1)} fusion(f32[24,2,256,1]{2,3,1,0:T(1,128)S(1)} %reshape.117, f32[24,2,128,256]{3,2,1,0:T(8,128)} %param.4), kind=kOutput, calls=%fused_computation.115 | convolution fusion | flops 18874368 | bytes 6352896 | tf_op jit(solution)/shard_map/tkij,tkj->ti/dot_general | solution.py:62
  253.2 0.7 multiply_reduce_fusion.6
  253.9 5.1 %fusion.77 = f32[24,1,2,256]{3,1,2,0:T(1,128)S(1)} fusion(f32[24,128,1,1]{1,2,3,0:T(1,128)S(1)} %bitcast.88, f32[24,2,128,256]{3,2,1,0:T(8,128)} %param.4), kind=kOutput, calls=%fused_computation.116 | convolution fusion | flops 18874368 | bytes 6352896 | tf_op jit(solution)/shard_map/tkij,ti->tkj/dot_general | solution.py:70
  259.4 1.3 collective-permute-start.14
  260.7 5.3 %collective-permute-start.15 = (f32[48,256]{1,0:T(8,128)S(1)}, f32[48,256]{1,0:T(8,128)S(1)}, u32[]{:S(2)}, u32[]{:S(2)}) collective-permute-start(f32[48,256]{1,0:T(8,128)S(1)} %get-tuple-element.35), channel_id=1, source_target_pairs={{0,4},{4,8},{8,12},{12,16},{16,20},{20,24},{24,28},{1,5},{5,9},{9,... | collective-permute-start | bytes 147464 | tf_op jit(solution)/shard_map/ppermute | solution.py:29
  266.1 1.6 collective-permute-done.15
  267.7 7.8 %fusion.4 = f32[16,256]{1,0:T(8,128)S(1)} fusion(f32[48,256]{1,0:T(8,128)S(1)} %fusion.29), kind=kCustom, calls=%all-reduce-scatter.4 | all-reduce-scatter fusion | flops 16385 | bytes 66048
  275.6 1.3 collective-permute-start.22
  276.8 0.8 collective-permute-done.22
  277.8 0.7 fusion.50
  278.5 45.4 %all-reduce.10 = (f32[]{:T(128)}, f32[]{:T(128)}, f32[]{:T(128)}) all-reduce(f32[]{:T(128)} %get-tuple-element.23, f32[]{:T(128)} %get-tuple-element.3, f32[]{:T(128)} %get-tuple-element.2), channel_id=1, replica_groups=mesh['slab'=8,'sub'=4] {'slab','sub'}, use_global_device_ids=true, to_apply=%region_19.20 | all-reduce | flops 3 | bytes 24 | tf_op jit(solution)/shard_map/psum | solution.py:85
  325.9 5.7 %all-gather.3 = f32[4,12,256]{2,1,0:T(8,128)S(1)} all-gather(f32[1,12,256]{2,1,0:T(8,128)S(1)} %bitcast.85), channel_id=1, replica_groups=mesh['slab'=8,'sub'=4] {'sub'}, dimensions={0}, use_global_device_ids=true | all-gather | bytes 61440 | tf_op jit(solution)/shard_map/all_gather | solution.py:48
  331.5 1.5 collective-permute-start.17
  333.0 4.4 %collective-permute-start.16 = (f32[48,256]{1,0:T(8,128)S(1)}, f32[48,256]{1,0:T(8,128)S(1)}, u32[]{:S(2)}, u32[]{:S(2)}) collective-permute-start(f32[48,256]{1,0:T(8,128)S(1)} %reshape.93), channel_id=1, source_target_pairs={{0,4},{4,8},{8,12},{12,16},{16,20},{20,24},{24,28},{1,5},{5,9},{9,... | collective-permute-start | bytes 147464 | tf_op jit(solution)/shard_map/ppermute | solution.py:18
  337.7 1.4 collective-permute-done.16
  339.4 7.3 %fusion.78 = f32[24,1,128,1]{2,1,3,0:T(1,128)S(1)} fusion(f32[24,2,256,1]{2,3,1,0:T(1,128)S(1)} %reshape.119, f32[24,2,128,256]{3,2,1,0:T(8,128)} %param.4), kind=kOutput, calls=%fused_computation.117 | convolution fusion | flops 18874368 | bytes 6352896 | tf_op jit(solution)/shard_map/tkij,tkj->ti/dot_general | solution.py:62
  346.7 0.7 multiply_reduce_fusion.5
  347.4 42.3 %psum.87 = f32[]{:T(128)} all-reduce(f32[]{:T(128)} %multiply_reduce_fusion.5), channel_id=1, replica_groups=mesh['slab'=8,'sub'=4] {'slab','sub'}, use_global_device_ids=true, to_apply=%region_26.27 | all-reduce | flops 1 | bytes 8 | tf_op jit(solution)/shard_map/psum | solution.py:85
  (73 shorter events, 7.2 us)
Async XLA Ops:
  3.0 37.4 %copy-start.1 = (u32[32]{0:T(128)S(1)}, u32[32]{0:T(128)}, u32[]{:S(2)}) copy-start(u32[32]{0:T(128)} %constant.62) | copy-start | bytes 388
  8.5 17.6 %collective-permute-start = (f32[48,256]{1,0:T(8,128)S(1)}, f32[48,256]{1,0:T(8,128)S(1)}, u32[]{:S(2)}, u32[]{:S(2)}) collective-permute-start(f32[48,256]{1,0:T(8,128)S(1)} %get-tuple-element.42), channel_id=1, source_target_pairs={{4,0},{8,4},{12,8},{16,12},{20,16},{24,20},{28,24},{5,1},{9,5},{13... | collective-permute-start | bytes 147464 | tf_op jit(solution)/shard_map/ppermute | solution.py:29
  9.8 16.4 %collective-permute-start.1 = (f32[48,256]{1,0:T(8,128)S(1)}, f32[48,256]{1,0:T(8,128)S(1)}, u32[]{:S(2)}, u32[]{:S(2)}) collective-permute-start(f32[48,256]{1,0:T(8,128)S(1)} %get-tuple-element.43), channel_id=1, source_target_pairs={{0,4},{4,8},{8,12},{12,16},{16,20},{20,24},{24,28},{1,5},{5,9},{9,... | collective-permute-start | bytes 147464 | tf_op jit(solution)/shard_map/ppermute | solution.py:29
  19.4 6.9 %collective-permute-start.2 = (f32[48,256]{1,0:T(8,128)S(1)}, f32[48,256]{1,0:T(8,128)S(1)}, u32[]{:S(2)}, u32[]{:S(2)}) collective-permute-start(f32[48,256]{1,0:T(8,128)S(1)} %get-tuple-element.40), channel_id=1, source_target_pairs={{4,0},{8,4},{12,8},{16,12},{20,16},{24,20},{28,24},{5,1},{9,5},{13... | collective-permute-start | bytes 147464 | tf_op jit(solution)/shard_map/ppermute | solution.py:29
  20.7 7.2 %collective-permute-start.3 = (f32[48,256]{1,0:T(8,128)S(1)}, f32[48,256]{1,0:T(8,128)S(1)}, u32[]{:S(2)}, u32[]{:S(2)}) collective-permute-start(f32[48,256]{1,0:T(8,128)S(1)} %get-tuple-element.41), channel_id=1, source_target_pairs={{0,4},{4,8},{8,12},{12,16},{16,20},{20,24},{24,28},{1,5},{5,9},{9,... | collective-permute-start | bytes 147464 | tf_op jit(solution)/shard_map/ppermute | solution.py:29
  34.7 7.0 %collective-permute-start.19 = (f32[12,256]{1,0:T(8,128)S(1)}, f32[12,256]{1,0:T(8,128)S(1)}, u32[]{:S(2)}, u32[]{:S(2)}) collective-permute-start(f32[12,256]{1,0:T(8,128)S(1)} %slice.91), channel_id=1, source_target_pairs={{0,1},{1,2},{2,3},{4,5},{5,6},{6,7},{8,9},{9,10},{10,11},{12,13},{... | collective-permute-start | bytes 36872
  36.2 5.6 %collective-permute-start.18 = (f32[12,256]{1,0:T(8,128)S(1)}, f32[12,256]{1,0:T(8,128)S(1)}, u32[]{:S(2)}, u32[]{:S(2)}) collective-permute-start(f32[12,256]{1,0:T(8,128)S(1)} %slice.90), channel_id=1, source_target_pairs={{0,1},{1,2},{2,3},{4,5},{5,6},{6,7},{8,9},{9,10},{10,11},{12,13},{... | collective-permute-start | bytes 36872
  47.2 7.1 %collective-permute-start.5 = (f32[48,256]{1,0:T(8,128)S(1)}, f32[48,256]{1,0:T(8,128)S(1)}, u32[]{:S(2)}, u32[]{:S(2)}) collective-permute-start(f32[48,256]{1,0:T(8,128)S(1)} %reshape.87), channel_id=1, source_target_pairs={{4,0},{8,4},{12,8},{16,12},{20,16},{24,20},{28,24},{5,1},{9,5},{13... | collective-permute-start | bytes 147464 | tf_op jit(solution)/shard_map/ppermute | solution.py:21
  48.5 7.6 %collective-permute-start.4 = (f32[48,256]{1,0:T(8,128)S(1)}, f32[48,256]{1,0:T(8,128)S(1)}, u32[]{:S(2)}, u32[]{:S(2)}) collective-permute-start(f32[48,256]{1,0:T(8,128)S(1)} %reshape.87), channel_id=1, source_target_pairs={{0,4},{4,8},{8,12},{12,16},{16,20},{20,24},{24,28},{1,5},{5,9},{9,... | collective-permute-start | bytes 147464 | tf_op jit(solution)/shard_map/ppermute | solution.py:18
  69.9 6.8 %collective-permute-start.6 = (f32[48,256]{1,0:T(8,128)S(1)}, f32[48,256]{1,0:T(8,128)S(1)}, u32[]{:S(2)}, u32[]{:S(2)}) collective-permute-start(f32[48,256]{1,0:T(8,128)S(1)} %get-tuple-element.38), channel_id=1, source_target_pairs={{4,0},{8,4},{12,8},{16,12},{20,16},{24,20},{28,24},{5,1},{9,5},{13... | collective-permute-start | bytes 147464 | tf_op jit(solution)/shard_map/ppermute | solution.py:29
  71.2 7.1 %collective-permute-start.7 = (f32[48,256]{1,0:T(8,128)S(1)}, f32[48,256]{1,0:T(8,128)S(1)}, u32[]{:S(2)}, u32[]{:S(2)}) collective-permute-start(f32[48,256]{1,0:T(8,128)S(1)} %get-tuple-element.39), channel_id=1, source_target_pairs={{0,4},{4,8},{8,12},{12,16},{16,20},{20,24},{24,28},{1,5},{5,9},{9,... | collective-permute-start | bytes 147464 | tf_op jit(solution)/shard_map/ppermute | solution.py:29
  86.0 2.1 collective-permute-start.20
  144.5 6.0 %collective-permute-start.9 = (f32[48,256]{1,0:T(8,128)S(1)}, f32[48,256]{1,0:T(8,128)S(1)}, u32[]{:S(2)}, u32[]{:S(2)}) collective-permute-start(f32[48,256]{1,0:T(8,128)S(1)} %reshape.89), channel_id=1, source_target_pairs={{4,0},{8,4},{12,8},{16,12},{20,16},{24,20},{28,24},{5,1},{9,5},{13... | collective-permute-start | bytes 147464 | tf_op jit(solution)/shard_map/ppermute | solution.py:21
  145.8 6.3 %collective-permute-start.8 = (f32[48,256]{1,0:T(8,128)S(1)}, f32[48,256]{1,0:T(8,128)S(1)}, u32[]{:S(2)}, u32[]{:S(2)}) collective-permute-start(f32[48,256]{1,0:T(8,128)S(1)} %reshape.89), channel_id=1, source_target_pairs={{0,4},{4,8},{8,12},{12,16},{16,20},{20,24},{24,28},{1,5},{5,9},{9,... | collective-permute-start | bytes 147464 | tf_op jit(solution)/shard_map/ppermute | solution.py:18
  165.8 6.7 %collective-permute-start.10 = (f32[48,256]{1,0:T(8,128)S(1)}, f32[48,256]{1,0:T(8,128)S(1)}, u32[]{:S(2)}, u32[]{:S(2)}) collective-permute-start(f32[48,256]{1,0:T(8,128)S(1)} %get-tuple-element.36), channel_id=1, source_target_pairs={{4,0},{8,4},{12,8},{16,12},{20,16},{24,20},{28,24},{5,1},{9,5},{13... | collective-permute-start | bytes 147464 | tf_op jit(solution)/shard_map/ppermute | solution.py:29
  167.1 7.0 %collective-permute-start.11 = (f32[48,256]{1,0:T(8,128)S(1)}, f32[48,256]{1,0:T(8,128)S(1)}, u32[]{:S(2)}, u32[]{:S(2)}) collective-permute-start(f32[48,256]{1,0:T(8,128)S(1)} %get-tuple-element.37), channel_id=1, source_target_pairs={{0,4},{4,8},{8,12},{12,16},{16,20},{20,24},{24,28},{1,5},{5,9},{9,... | collective-permute-start | bytes 147464 | tf_op jit(solution)/shard_map/ppermute | solution.py:29
  182.0 2.1 collective-permute-start.21
  238.1 6.0 %collective-permute-start.13 = (f32[48,256]{1,0:T(8,128)S(1)}, f32[48,256]{1,0:T(8,128)S(1)}, u32[]{:S(2)}, u32[]{:S(2)}) collective-permute-start(f32[48,256]{1,0:T(8,128)S(1)} %reshape.91), channel_id=1, source_target_pairs={{4,0},{8,4},{12,8},{16,12},{20,16},{24,20},{28,24},{5,1},{9,5},{13... | collective-permute-start | bytes 147464 | tf_op jit(solution)/shard_map/ppermute | solution.py:21
  239.4 6.3 %collective-permute-start.12 = (f32[48,256]{1,0:T(8,128)S(1)}, f32[48,256]{1,0:T(8,128)S(1)}, u32[]{:S(2)}, u32[]{:S(2)}) collective-permute-start(f32[48,256]{1,0:T(8,128)S(1)} %reshape.91), channel_id=1, source_target_pairs={{0,4},{4,8},{8,12},{12,16},{16,20},{20,24},{24,28},{1,5},{5,9},{9,... | collective-permute-start | bytes 147464 | tf_op jit(solution)/shard_map/ppermute | solution.py:18
  253.9 137.1 %copy-start = (f32[24,128]{1,0:T(8,128)S(1)}, f32[24,128]{1,0:T(8,128)}, u32[]{:S(2)}) copy-start(f32[24,128]{1,0:T(8,128)} %param.7) | copy-start | bytes 36868
  259.4 6.7 %collective-permute-start.14 = (f32[48,256]{1,0:T(8,128)S(1)}, f32[48,256]{1,0:T(8,128)S(1)}, u32[]{:S(2)}, u32[]{:S(2)}) collective-permute-start(f32[48,256]{1,0:T(8,128)S(1)} %get-tuple-element.34), channel_id=1, source_target_pairs={{4,0},{8,4},{12,8},{16,12},{20,16},{24,20},{28,24},{5,1},{9,5},{13... | collective-permute-start | bytes 147464 | tf_op jit(solution)/shard_map/ppermute | solution.py:29
  260.7 7.0 %collective-permute-start.15 = (f32[48,256]{1,0:T(8,128)S(1)}, f32[48,256]{1,0:T(8,128)S(1)}, u32[]{:S(2)}, u32[]{:S(2)}) collective-permute-start(f32[48,256]{1,0:T(8,128)S(1)} %get-tuple-element.35), channel_id=1, source_target_pairs={{0,4},{4,8},{8,12},{12,16},{16,20},{20,24},{24,28},{1,5},{5,9},{9,... | collective-permute-start | bytes 147464 | tf_op jit(solution)/shard_map/ppermute | solution.py:29
  275.6 2.1 collective-permute-start.22
  331.5 6.2 %collective-permute-start.17 = (f32[48,256]{1,0:T(8,128)S(1)}, f32[48,256]{1,0:T(8,128)S(1)}, u32[]{:S(2)}, u32[]{:S(2)}) collective-permute-start(f32[48,256]{1,0:T(8,128)S(1)} %reshape.93), channel_id=1, source_target_pairs={{4,0},{8,4},{12,8},{16,12},{20,16},{24,20},{28,24},{5,1},{9,5},{13... | collective-permute-start | bytes 147464 | tf_op jit(solution)/shard_map/ppermute | solution.py:21
  333.0 6.1 %collective-permute-start.16 = (f32[48,256]{1,0:T(8,128)S(1)}, f32[48,256]{1,0:T(8,128)S(1)}, u32[]{:S(2)}, u32[]{:S(2)}) collective-permute-start(f32[48,256]{1,0:T(8,128)S(1)} %reshape.93), channel_id=1, source_target_pairs={{0,4},{4,8},{8,12},{12,16},{16,20},{20,24},{24,28},{1,5},{5,9},{9,... | collective-permute-start | bytes 147464 | tf_op jit(solution)/shard_map/ppermute | solution.py:18
where the time goes:
time: 393 us; the launch traced here: 392 us
  blocking collectives  232 us (59%)
  starting transfers between devices  67.3 us (17%)
  matrix products  51.9 us (13%)
  waiting for transfers between devices  16.5 us (4%)
  other arithmetic  11.4 us (3%)
  between operations  11.1 us (3%)
    psum x3, blocking collectives, per_device(): lax.psum((jnp.sum(image * image), jnp.sum(scaled * back_image), jnp.sum(b...  133 us
    psum x1, blocking collectives, per_device(): rho_now = lax.psum(jnp.sum(normal_res * scaled), ('slab', 'sub'))  45.8 us
    ppermute x10, starting transfers between devices, from_behind(): return lax.ppermute(block, axis, route)  33.3 us
    unnamed x4, blocking collectives  30.1 us
    dot_general x4, matrix products, forward(): image = jnp.einsum('tkij,tkj->ti', values, picked, precision=precise)  29 us
    all_gather x4, blocking collectives, gather_window(): gathered = lax.all_gather(field, 'sub', axis=0, tiled=True)  22.3 us
    dot_general x4, matrix products, backward(): jnp.einsum('tkij,ti->tkj', values, rows, precision=precise)  20.3 us
    ppermute x4, starting transfers between devices, with_halo(): lax.ppermute(lax.slice_in_dim(block, block.shape[dim] - width, None, axis...  19.1 us
  transfers between devices with their start and end apart: 23, of which 18 were waited for; matrix products, arithmetic and copies ran while one was open for 1% of the time, Pallas kernels for 0%

commit v1 on v0

v1 whole, which is shorter than its diff:
```python
import functools

import jax
import jax.numpy as jnp
from jax import lax
from jax.experimental import pallas as pl
from jax.experimental.pallas import tpu as pltpu
from jax.sharding import PartitionSpec as P

ITERS = 4
NB_DEV = 12
LANES = 128
MESH = pl.DeviceIdType.MESH


def round_up(size, unit):
    return -(-size // unit) * unit


def kernel(
    n_slab,
    n_sub,
    values_hbm,
    ids_smem,
    counts_smem,
    right_ref,
    solution_ref,
    residual_ref,
    values,
    wid,
    turned,
    selector,
    terms,
    squares,
    image_cols,
    image_rows,
    first_out,
    first_in,
    part_out,
    part_in,
    field_out,
    field_in,
    scaled_win,
    direction_win,
    scal1,
    scal2,
    load_sem,
    first_send,
    first_recv,
    part_send,
    part_recv,
    field_send,
    field_recv,
    scal1_send,
    scal1_recv,
    scal2_send,
    scal2_recv,
):
    tiles, coupled, rows, block = values.shape
    halves = block // LANES
    held = NB_DEV * halves
    n = n_slab * n_sub
    window = 3 * n_sub * held
    f32 = jnp.float32
    slab = lax.axis_index("slab")
    sub = lax.axis_index("sub")
    me = slab * n_sub + sub

    for t in range(tiles):
        pltpu.make_async_copy(values_hbm.at[t], values.at[t], load_sem.at[t]).start()

    def other(j):
        target = lax.rem(me + j, n)
        return (lax.div(target, n_sub), lax.rem(target, n_sub))

    barrier = pltpu.get_barrier_semaphore()

    @pl.loop(1, n)
    def _(j):
        pl.semaphore_signal(barrier, inc=1, device_id=other(j), device_id_type=MESH)

    turned[...] = jnp.zeros_like(turned)
    terms[...] = jnp.zeros_like(terms)
    squares[...] = jnp.zeros_like(squares)
    lane_ids = lax.broadcasted_iota(jnp.int32, (1, turned.shape[1]), 1)

    @pl.loop(0, tiles)
    def _(t):
        for k in range(coupled):
            b = ids_smem[t, k]
            owner = lax.div(b, NB_DEV)
            rel = jnp.clip(lax.div(owner, n_sub) - slab + 1, 0, 2)
            row = (rel * n_sub + lax.rem(owner, n_sub)) * held + lax.rem(b, NB_DEV)
            wid[t, k] = row
            for h in range(halves):
                hot = (lane_ids == row + h * NB_DEV).astype(f32)
                turned[pl.ds((k * halves + h) * tiles + t, 1), :] = hot

    selector[...] = turned[...].T.astype(jnp.bfloat16)

    missing = ((slab == 0, 0, 1), (slab == n_slab - 1, 2, -1))
    for absent, rel, delta in missing:

        @pl.when(absent)
        def _(rel=rel, delta=delta):
            low = (delta + 1) * n_sub
            first_in[low : low + n_sub] = jnp.zeros((n_sub,) + first_in.shape[1:], f32)
            for it in range(part_in.shape[0]):
                part_in[it, low : low + n_sub] = jnp.zeros((n_sub,) + part_in.shape[2:], f32)
            for it in range(field_in.shape[0]):
                field_in[it, rel] = jnp.zeros(field_in.shape[2:], f32)

    def live(t):
        return jnp.where(t < counts_smem[0, 0], 1.0, 0.0).astype(f32)

    eye = (
        lax.broadcasted_iota(jnp.int32, (rows, LANES), 0)
        == lax.broadcasted_iota(jnp.int32, (rows, LANES), 1)
    ).astype(f32)

    def half(h):
        return slice(h * LANES, (h + 1) * LANES)

    def term_row(k, h, t):
        return pl.ds((k * halves + h) * tiles + t, 1)

    def scatter(term_refs):
        cut = []
        for ref in term_refs:
            rest = ref[...]
            for _ in range(3):
                piece = rest.astype(jnp.bfloat16)
                cut.append(piece)
                rest = rest - piece.astype(f32)
        spread = jnp.dot(
            selector[...], jnp.concatenate(cut, axis=1), preferred_element_type=f32
        )
        outs = []
        for i in range(len(term_refs)):
            a, b, c = (spread[:window, half(3 * i + j)] for j in range(3))
            outs.append((a + (b + c)).reshape(3, n_sub, held, LANES))
        return outs

    def partners():
        for ds in (1, -1, 0):
            for step in range(n_sub):
                if ds == 0 and step == 0:
                    continue
                exists = None
                if ds:
                    exists = slab + ds >= 0 if ds < 0 else slab + ds < n_slab
                source_exists = None
                if ds:
                    source_exists = slab - ds >= 0 if ds > 0 else slab - ds < n_slab
                yield ds, step, exists, source_exists

    def guarded(cond, act):
        if cond is None:
            act()
        else:
            pl.when(cond)(act)

    def part_copy(out_ref, in_ref, send, recv, ds, step):
        target = lax.rem(sub + step, n_sub)
        slot = (ds + 1) * n_sub + step
        return pltpu.make_async_remote_copy(
            src_ref=out_ref.at[ds + 1, target],
            dst_ref=in_ref.at[slot],
            send_sem=send.at[slot],
            recv_sem=recv.at[slot],
            device_id=(slab + ds, target),
            device_id_type=MESH,
        )

    def field_copy(it, ds, step):
        target = lax.rem(sub + step, n_sub)
        slot = (ds + 1) * n_sub + step
        return pltpu.make_async_remote_copy(
            src_ref=field_out.at[it],
            dst_ref=field_in.at[it, 1 - ds, sub],
            send_sem=field_send.at[it, slot],
            recv_sem=field_recv.at[it, slot],
            device_id=(slab + ds, target),
            device_id_type=MESH,
        )

    def start_all(copy):
        for ds, step, exists, _ in partners():
            guarded(exists, lambda ds=ds, step=step: copy(ds, step).start())

    def wait_recv_all(copy):
        for ds, step, _, source in partners():
            guarded(source, lambda ds=ds, step=step: copy(ds, step).wait_recv())

    def wait_send_all(copy):
        for ds, step, exists, _ in partners():
            guarded(exists, lambda ds=ds, step=step: copy(ds, step).wait_send())

    def scal_copy(ref, send, recv, it, j):
        return pltpu.make_async_remote_copy(
            src_ref=ref.at[it, me],
            dst_ref=ref.at[it, me],
            send_sem=send.at[it],
            recv_sem=recv.at[it],
            device_id=other(j),
            device_id_type=MESH,
        )

    def scal_start(ref, send, recv, it):
        @pl.loop(1, n)
        def _(j):
            scal_copy(ref, send, recv, it, j).start()

    def scal_all(ref, send, recv, it):
        rest = ref.at[it, pl.ds(0, n - 1)]
        return pltpu.make_async_remote_copy(
            src_ref=rest,
            dst_ref=rest,
            send_sem=send.at[it],
            recv_sem=recv.at[it],
            device_id=other(1),
            device_id_type=MESH,
        )

    def total(x):
        return jnp.sum(jnp.sum(x, axis=0, keepdims=True), axis=1, keepdims=True)

    @pl.loop(0, tiles)
    def _(t):
        pltpu.make_async_copy(values_hbm.at[t], values.at[t], load_sem.at[t]).wait()
        alive = live(t)
        cols = jnp.sum(eye * (right_ref[pl.ds(t, 1), :] * alive), axis=1, keepdims=True)
        cols = jnp.broadcast_to(cols, (rows, LANES))
        for k in range(coupled):
            for h in range(halves):
                a = values[t, k, :, half(h)]
                terms[term_row(k, h, t), :] = jnp.sum(a * cols, axis=0, keepdims=True)
                squares[term_row(k, h, t), :] = (
                    jnp.sum(a * a, axis=0, keepdims=True) * alive
                )
        residual_ref[pl.ds(t, 1), :] = right_ref[pl.ds(t, 1), :] * alive

    pieces = scatter((terms, squares))
    for i in range(2):
        first_out[:, :, i] = pieces[i]
    pl.semaphore_wait(barrier, n - 1)
    first_copy = functools.partial(part_copy, first_out, first_in, first_send, first_recv)
    start_all(first_copy)
    wait_recv_all(first_copy)
    sums = first_out[1, sub]
    for slot in range(3 * n_sub):
        if slot != n_sub:
            sums = sums + first_in[slot]
    normal_res = sums[0]
    jacobi = 1.0 / (1.0 + sums[1])
    scaled = jacobi * normal_res
    field_out[0] = scaled
    rho_part = total(normal_res * scaled)
    scal2[0, me] = jnp.broadcast_to(rho_part, (2, LANES))
    scal_start(scal2, scal2_send, scal2_recv, 0)
    start_all(functools.partial(field_copy, 0))
    field_in[0, 1, sub] = scaled
    wait_recv_all(functools.partial(field_copy, 0))
    scaled_win[...] = field_in[0].reshape(window, LANES)
    direction_win[...] = scaled_win[...]
    scal_all(scal2, scal2_send, scal2_recv, 0).wait_recv()
    rho_now = jnp.sum(scal2[0], axis=0)[0:1]

    answer = jnp.zeros((held, LANES), f32)
    own_rows = pl.ds(pl.multiple_of((n_sub + sub) * held, 8), held)
    for it in range(ITERS):
        last = it == ITERS - 1

        def tile_pass(t, norm):
            alive = live(t)
            m = None
            for k in range(coupled):
                for h in range(halves):
                    picked = direction_win[pl.ds(wid[t, k] + h * NB_DEV, 1), :] * alive
                    product = values[t, k, :, half(h)] * picked
                    m = product if m is None else m + product
            image = jnp.broadcast_to(jnp.sum(m, axis=1, keepdims=True), (rows, LANES))
            image_cols[t] = image
            if not last:
                for k in range(coupled):
                    for h in range(halves):
                        terms[term_row(k, h, t), :] = jnp.sum(
                            values[t, k, :, half(h)] * image, axis=0, keepdims=True
                        )
            return norm + jnp.sum(image * image, axis=0, keepdims=True)

        norm = lax.fori_loop(0, tiles, tile_pass, jnp.zeros((1, LANES), f32), unroll=2)
        scal1[it, me] = norm
        if not last:
            part_out[it] = scatter((terms,))[0]
            out_copy = functools.partial(
                part_copy, part_out.at[it], part_in.at[it], part_send.at[it], part_recv.at[it]
            )
            start_all(out_copy)
        scal_start(scal1, scal1_send, scal1_recv, it)

        @pl.loop(0, tiles)
        def _(t):
            image_rows[pl.ds(t, 1), :] = jnp.sum(image_cols[t] * eye, axis=0, keepdims=True)

        if not last:
            wait_recv_all(out_copy)
            back = part_out[it, 1, sub]
            for slot in range(3 * n_sub):
                if slot != n_sub:
                    back = back + part_in[it, slot]
            back_scaled = jacobi * back
            field_out[it + 1] = back_scaled
            scal2[it + 1, me, 0:1] = jnp.broadcast_to(total(scaled * back), (1, LANES))
            scal2[it + 1, me, 1:2] = jnp.broadcast_to(total(back * back_scaled), (1, LANES))
            scal_start(scal2, scal2_send, scal2_recv, it + 1)
            start_all(functools.partial(field_copy, it + 1))
            field_in[it + 1, 1, sub] = back_scaled
        scal_all(scal1, scal1_send, scal1_recv, it).wait_recv()
        step_size = rho_now / jnp.sum(scal1[it], axis=0)
        answer = answer + step_size * direction_win[own_rows, :]
        residual_ref[...] = residual_ref[...] - step_size * image_rows[...]
        if not last:
            scaled = scaled - step_size * back_scaled
            wait_recv_all(functools.partial(field_copy, it + 1))
            scaled_win[...] = scaled_win[...] - step_size * field_in[it + 1].reshape(window, LANES)
            scal_all(scal2, scal2_send, scal2_recv, it + 1).wait_recv()
            both = jnp.sum(scal2[it + 1], axis=0)
            rho_next = rho_now - 2.0 * step_size * both[0:1] + step_size * step_size * both[1:2]
            direction_win[...] = scaled_win[...] + (rho_next / rho_now) * direction_win[...]
            rho_now = rho_next

    for h in range(halves):
        solution_ref[:, half(h)] = answer[h * NB_DEV : (h + 1) * NB_DEV]

    wait_send_all(first_copy)
    for it in range(ITERS):
        wait_send_all(functools.partial(field_copy, it))
        scal_all(scal1, scal1_send, scal1_recv, it).wait_send()
        scal_all(scal2, scal2_send, scal2_recv, it).wait_send()
        if it < ITERS - 1:
            wait_send_all(
                functools.partial(
                    part_copy, part_out.at[it], part_in.at[it], part_send.at[it], part_recv.at[it]
                )
            )


def per_device(n_slab, n_sub, values, block_ids, tile_counts, right_side):
    tiles, coupled, rows, block = values.shape
    halves = block // LANES
    held = NB_DEV * halves
    n = n_slab * n_sub
    slots = 3 * n_sub
    window = slots * held
    n_terms = round_up(tiles * coupled * halves, LANES)
    n_window = round_up(window, LANES)
    f32 = jnp.float32
    vmem = pltpu.VMEM
    dma = pltpu.SemaphoreType.DMA
    whole = pl.BlockSpec(memory_space=pltpu.VMEM)
    scalars = pl.BlockSpec(memory_space=pltpu.SMEM)
    return pl.pallas_call(
        functools.partial(kernel, n_slab, n_sub),
        out_shape=(
            jax.ShapeDtypeStruct((NB_DEV, block), f32),
            jax.ShapeDtypeStruct((tiles, rows), f32),
        ),
        in_specs=[pl.BlockSpec(memory_space=pl.ANY), scalars, scalars, whole],
        out_specs=(whole, whole),
        scratch_shapes=[
            vmem(values.shape, f32),
            pltpu.SMEM((tiles, coupled), jnp.int32),
            vmem((n_terms, n_window), f32),
            vmem((n_window, n_terms), jnp.bfloat16),
            vmem((n_terms, LANES), f32),
            vmem((n_terms, LANES), f32),
            vmem((tiles, rows, LANES), f32),
            vmem((tiles, LANES), f32),
            vmem((3, n_sub, 2, held, LANES), f32),
            vmem((slots, 2, held, LANES), f32),
            vmem((ITERS - 1, 3, n_sub, held, LANES), f32),
            vmem((ITERS - 1, slots, held, LANES), f32),
            vmem((ITERS, held, LANES), f32),
            vmem((ITERS, 3, n_sub, held, LANES), f32),
            vmem((window, LANES), f32),
            vmem((window, LANES), f32),
            vmem((ITERS, n, 1, LANES), f32),
            vmem((ITERS, n, 2, LANES), f32),
            dma((tiles,)),
            dma((slots,)),
            dma((slots,)),
            dma((ITERS - 1, slots)),
            dma((ITERS - 1, slots)),
            dma((ITERS, slots)),
            dma((ITERS, slots)),
            dma((ITERS,)),
            dma((ITERS,)),
            dma((ITERS,)),
            dma((ITERS,)),
        ],
        compiler_params=pltpu.CompilerParams(
            collective_id=0, has_side_effects=True, vmem_limit_bytes=48 * 1024 * 1024
        ),
    )(values, block_ids, tile_counts, right_side)


def solution(mesh):
    in_specs = (
        P(("slab", "sub"), None, None, None),
        P(("slab", "sub"), None),
        P("slab", "sub"),
        P(("slab", "sub"), None),
    )
    out_specs = (P(("slab", "sub"), None), P(("slab", "sub"), None))
    return jax.shard_map(
        functools.partial(per_device, mesh.shape["slab"], mesh.shape["sub"]),
        mesh=mesh,
        in_specs=in_specs,
        out_specs=out_specs,
        check_vma=False,
    )
```

time: 393 us -> 66.9 us (0.17)
  blocking collectives: 232 us -> 0 us
  starting transfers between devices: 67.3 us -> 0 us
  Pallas kernels: 0 us -> 62.6 us
  matrix products: 51.9 us -> 0 us
  waiting for transfers between devices: 16.5 us -> 0 us
  other arithmetic: 11.4 us -> 0 us
  between operations: 11.1 us -> 1.29 us
    psum x4 -> x0, blocking collectives: 179 us -> none  [the longest x3 133 us: per_device(): lax.psum((jnp.sum(image * image), jnp.sum(scaled * back_image), jnp.sum(b...]
    pallas_call x0 -> x1, Pallas kernels: none -> 62.6 us  [per_device(): pl.pallas_call(functools.partial(kernel, n_slab, n_sub), out_shape=(jax.S...]
    ppermute x18 -> x0, starting transfers between devices: 57.8 us -> none  [the longest x10 33.3 us: from_behind(): return lax.ppermute(block, axis, route)]
    dot_general x17 -> x0, matrix products: 51.9 us -> none  [the longest x4 29 us: forward(): image = jnp.einsum('tkij,tkj->ti', values, picked, precision=precise)]
    unnamed x4 -> x0, blocking collectives: 30.1 us -> none
    all_gather x4 -> x0, blocking collectives: 22.3 us -> none  [gather_window(): gathered = lax.all_gather(field, 'sub', axis=0, tiled=True)]
    ppermute x18 -> x0, waiting for transfers between devices: 14 us -> none  [the longest x10 6.89 us: from_behind(): return lax.ppermute(block, axis, route)]
    unnamed x5 -> x0, starting transfers between devices: 9.58 us -> none
  transfers between devices with their start and end apart: 23 -> 0, of which waited for: 18 -> 0; matrix products, arithmetic and copies ran while one was open for 1% -> 0% of each run, Pallas kernels for 0% -> 0%
where the time goes in v1:
time: 66.9 us; the launch traced here: 66.6 us
  Pallas kernels  62.6 us (94%)
  local copies, waits for them, and re-layouts  2.67 us (4%)
  between operations  1.29 us (2%)
    pallas_call x1, Pallas kernels, per_device(): pl.pallas_call(functools.partial(kernel, n_slab, n_sub), out_shape=(jax.S...  62.6 us
    unnamed x5, local copies, waits for them, and re-layouts  2.67 us

profile of v1, /device:TPU:0, one launch (start us, length us, event | category | flops | bytes accessed | tf_op | source)
XLA Modules:
  0.0 66.6 jit_solution(9848150717697762864)
XLA Ops:
  1.3 0.8 %copy.6.ids_smem = s32[24,2]{1,0:T(8,128)S(1)} copy(s32[24,2]{0,1:T(2,128)} %param.5) | data formatting | bytes 384 | tf_op args[1]
  2.0 0.0 copy-start
  2.0 0.7 %copy-done = f32[24,128]{1,0:T(8,128)S(1)} copy-done((f32[24,128]{1,0:T(8,128)S(1)}, f32[24,128]{1,0:T(8,128)}, u32[]{:S(2)}) %copy-start) | copy-done | bytes 12312
  2.7 62.6 %shard_map.59 = (f32[12,256]{1,0:T(8,128)S(1)}, f32[24,128]{1,0:T(8,128)S(1)}) custom-call(f32[24,2,128,256]{3,2,1,0:T(8,128)} %values_hbm.1, s32[24,2]{1,0:T(8,128)S(1)} %copy.6.ids_smem, s32[1,1]{1,0:T(1,128)S(6)} %copy.9.counts_smem, f32[24,128]{1,0:T(8,128)S(1)} %copy-done), custom_call_target="tpu_custom_call" | custom-call | tf_op jit(solution)/shard_map/pallas_call | solution.py:363
  65.4 0.6 copy.10
  66.0 0.6 copy.11
Async XLA Ops:
  2.0 0.7 %copy-start = (f32[24,128]{1,0:T(8,128)S(1)}, f32[24,128]{1,0:T(8,128)}, u32[]{:S(2)}) copy-start(f32[24,128]{1,0:T(8,128)} %right_ref.1) | copy-start | bytes 36868

commit v2 on v1

--- a/solution.py
+++ b/solution.py
@@ -21,9 +21,9 @@
     n_slab,
     n_sub,
     values_hbm,
-    ids_smem,
-    counts_smem,
-    right_ref,
+    ids_hbm,
+    counts_hbm,
+    right_hbm,
     solution_ref,
     residual_ref,
     values,
@@ -44,6 +44,10 @@
     direction_win,
     scal1,
     scal2,
+    ids_smem,
+    counts_smem,
+    right_ref,
+    small_sem,
     load_sem,
     first_send,
     first_recv,
@@ -66,6 +70,19 @@
     sub = lax.axis_index("sub")
     me = slab * n_sub + sub
 
+    def keeper(s):
+        return s + 1 - 2 * lax.rem(s, 2) if n_slab % 2 == 0 else s
+
+    kept = keeper(slab)
+
+    small = [
+        pltpu.make_async_copy(src, dst, small_sem.at[i])
+        for i, (src, dst) in enumerate(
+            ((ids_hbm, ids_smem), (counts_hbm, counts_smem), (right_hbm, right_ref))
+        )
+    ]
+    for copy in small:
+        copy.start()
     for t in range(tiles):
         pltpu.make_async_copy(values_hbm.at[t], values.at[t], load_sem.at[t]).start()
 
@@ -78,6 +95,9 @@
     @pl.loop(1, n)
     def _(j):
         pl.semaphore_signal(barrier, inc=1, device_id=other(j), device_id_type=MESH)
+
+    for copy in small:
+        copy.wait()
 
     turned[...] = jnp.zeros_like(turned)
     terms[...] = jnp.zeros_like(terms)
@@ -98,17 +118,19 @@
 
     selector[...] = turned[...].T.astype(jnp.bfloat16)
 
-    missing = ((slab == 0, 0, 1), (slab == n_slab - 1, 2, -1))
-    for absent, rel, delta in missing:
-
-        @pl.when(absent)
-        def _(rel=rel, delta=delta):
-            low = (delta + 1) * n_sub
-            first_in[low : low + n_sub] = jnp.zeros((n_sub,) + first_in.shape[1:], f32)
-            for it in range(part_in.shape[0]):
-                part_in[it, low : low + n_sub] = jnp.zeros((n_sub,) + part_in.shape[2:], f32)
-            for it in range(field_in.shape[0]):
-                field_in[it, rel] = jnp.zeros(field_in.shape[2:], f32)
+    def blank_part(low):
+        first_in[low : low + n_sub] = jnp.zeros((n_sub,) + first_in.shape[1:], f32)
+        for it in range(part_in.shape[0]):
+            part_in[it, low : low + n_sub] = jnp.zeros((n_sub,) + part_in.shape[2:], f32)
+
+    def blank_field(rel):
+        for it in range(field_in.shape[0]):
+            field_in[it, rel] = jnp.zeros(field_in.shape[2:], f32)
+
+    pl.when(kept == 0)(lambda: blank_part(2 * n_sub))
+    pl.when(kept == n_slab - 1)(lambda: blank_part(0))
+    pl.when(slab == 0)(lambda: blank_field(0))
+    pl.when(slab == n_slab - 1)(lambda: blank_field(2))
 
     def live(t):
         return jnp.where(t < counts_smem[0, 0], 1.0, 0.0).astype(f32)
@@ -141,24 +163,19 @@
             outs.append((a + (b + c)).reshape(3, n_sub, held, LANES))
         return outs
 
-    def partners():
+    def inside(s):
+        return jnp.logical_and(s >= 0, s < n_slab)
+
+    def each(act, scatters):
         for ds in (1, -1, 0):
             for step in range(n_sub):
-                if ds == 0 and step == 0:
-                    continue
-                exists = None
-                if ds:
-                    exists = slab + ds >= 0 if ds < 0 else slab + ds < n_slab
-                source_exists = None
-                if ds:
-                    source_exists = slab - ds >= 0 if ds > 0 else slab - ds < n_slab
-                yield ds, step, exists, source_exists
-
-    def guarded(cond, act):
-        if cond is None:
-            act()
-        else:
-            pl.when(cond)(act)
+                if scatters:
+                    exists, far = inside(slab + ds), keeper(slab + ds)
+                else:
+                    exists, far = inside(kept - ds), kept - ds
+                if step == 0:
+                    exists = jnp.logical_and(exists, far != slab)
+                pl.when(exists)(functools.partial(act, ds, step))
 
     def part_copy(out_ref, in_ref, send, recv, ds, step):
         target = lax.rem(sub + step, n_sub)
@@ -168,7 +185,7 @@
             dst_ref=in_ref.at[slot],
             send_sem=send.at[slot],
             recv_sem=recv.at[slot],
-            device_id=(slab + ds, target),
+            device_id=(keeper(slab + ds), target),
             device_id_type=MESH,
         )
 
@@ -177,24 +194,24 @@
         slot = (ds + 1) * n_sub + step
         return pltpu.make_async_remote_copy(
             src_ref=field_out.at[it],
-            dst_ref=field_in.at[it, 1 - ds, sub],
+            dst_ref=field_in.at[it, ds + 1, sub],
             send_sem=field_send.at[it, slot],
             recv_sem=field_recv.at[it, slot],
-            device_id=(slab + ds, target),
+            device_id=(kept - ds, target),
             device_id_type=MESH,
         )
 
-    def start_all(copy):
-        for ds, step, exists, _ in partners():
-            guarded(exists, lambda ds=ds, step=step: copy(ds, step).start())
-
-    def wait_recv_all(copy):
-        for ds, step, _, source in partners():
-            guarded(source, lambda ds=ds, step=step: copy(ds, step).wait_recv())
-
-    def wait_send_all(copy):
-        for ds, step, exists, _ in partners():
-            guarded(exists, lambda ds=ds, step=step: copy(ds, step).wait_send())
+    def start_all(copy, scatters):
+        each(lambda ds, step: copy(ds, step).start(), scatters)
+
+    def wait_recv_all(copy, scatters):
+        each(lambda ds, step: copy(ds, step).wait_recv(), not scatters)
+
+    def wait_send_all(copy, scatters):
+        each(lambda ds, step: copy(ds, step).wait_send(), scatters)
+
+    own_rel = kept - slab + 1
+    own_slot = own_rel * n_sub
 
     def scal_copy(ref, send, recv, it, j):
         return pltpu.make_async_remote_copy(
@@ -245,12 +262,10 @@
         first_out[:, :, i] = pieces[i]
     pl.semaphore_wait(barrier, n - 1)
     first_copy = functools.partial(part_copy, first_out, first_in, first_send, first_recv)
-    start_all(first_copy)
-    wait_recv_all(first_copy)
-    sums = first_out[1, sub]
-    for slot in range(3 * n_sub):
-        if slot != n_sub:
-            sums = sums + first_in[slot]
+    start_all(first_copy, True)
+    first_in[own_slot] = first_out[own_rel, sub]
+    wait_recv_all(first_copy, True)
+    sums = jnp.sum(first_in[...], axis=0)
     normal_res = sums[0]
     jacobi = 1.0 / (1.0 + sums[1])
     scaled = jacobi * normal_res
@@ -258,9 +273,9 @@
     rho_part = total(normal_res * scaled)
     scal2[0, me] = jnp.broadcast_to(rho_part, (2, LANES))
     scal_start(scal2, scal2_send, scal2_recv, 0)
-    start_all(functools.partial(field_copy, 0))
-    field_in[0, 1, sub] = scaled
-    wait_recv_all(functools.partial(field_copy, 0))
+    start_all(functools.partial(field_copy, 0), False)
+    field_in[0, own_rel, sub] = scaled
+    wait_recv_all(functools.partial(field_copy, 0), False)
     scaled_win[...] = field_in[0].reshape(window, LANES)
     direction_win[...] = scaled_win[...]
     scal_all(scal2, scal2_send, scal2_recv, 0).wait_recv()
@@ -296,7 +311,8 @@
             out_copy = functools.partial(
                 part_copy, part_out.at[it], part_in.at[it], part_send.at[it], part_recv.at[it]
             )
-            start_all(out_copy)
+            part_in[it, own_slot] = part_out[it, own_rel, sub]
+            start_all(out_copy, True)
         scal_start(scal1, scal1_send, scal1_recv, it)
 
         @pl.loop(0, tiles)
@@ -304,25 +320,22 @@
             image_rows[pl.ds(t, 1), :] = jnp.sum(image_cols[t] * eye, axis=0, keepdims=True)
 
         if not last:
-            wait_recv_all(out_copy)
-            back = part_out[it, 1, sub]
-            for slot in range(3 * n_sub):
-                if slot != n_sub:
-                    back = back + part_in[it, slot]
+            wait_recv_all(out_copy, True)
+            back = jnp.sum(part_in[it], axis=0)
             back_scaled = jacobi * back
             field_out[it + 1] = back_scaled
             scal2[it + 1, me, 0:1] = jnp.broadcast_to(total(scaled * back), (1, LANES))
             scal2[it + 1, me, 1:2] = jnp.broadcast_to(total(back * back_scaled), (1, LANES))
             scal_start(scal2, scal2_send, scal2_recv, it + 1)
-            start_all(functools.partial(field_copy, it + 1))
-            field_in[it + 1, 1, sub] = back_scaled
+            start_all(functools.partial(field_copy, it + 1), False)
+            field_in[it + 1, own_rel, sub] = back_scaled
         scal_all(scal1, scal1_send, scal1_recv, it).wait_recv()
         step_size = rho_now / jnp.sum(scal1[it], axis=0)
         answer = answer + step_size * direction_win[own_rows, :]
         residual_ref[...] = residual_ref[...] - step_size * image_rows[...]
         if not last:
             scaled = scaled - step_size * back_scaled
-            wait_recv_all(functools.partial(field_copy, it + 1))
+            wait_recv_all(functools.partial(field_copy, it + 1), False)
             scaled_win[...] = scaled_win[...] - step_size * field_in[it + 1].reshape(window, LANES)
             scal_all(scal2, scal2_send, scal2_recv, it + 1).wait_recv()
             both = jnp.sum(scal2[it + 1], axis=0)
@@ -333,16 +346,17 @@
     for h in range(halves):
         solution_ref[:, half(h)] = answer[h * NB_DEV : (h + 1) * NB_DEV]
 
-    wait_send_all(first_copy)
+    wait_send_all(first_copy, True)
     for it in range(ITERS):
-        wait_send_all(functools.partial(field_copy, it))
+        wait_send_all(functools.partial(field_copy, it), False)
         scal_all(scal1, scal1_send, scal1_recv, it).wait_send()
         scal_all(scal2, scal2_send, scal2_recv, it).wait_send()
         if it < ITERS - 1:
             wait_send_all(
                 functools.partial(
                     part_copy, part_out.at[it], part_in.at[it], part_send.at[it], part_recv.at[it]
-                )
+                ),
+                True,
             )
 
 
@@ -359,14 +373,13 @@
     vmem = pltpu.VMEM
     dma = pltpu.SemaphoreType.DMA
     whole = pl.BlockSpec(memory_space=pltpu.VMEM)
-    scalars = pl.BlockSpec(memory_space=pltpu.SMEM)
     return pl.pallas_call(
         functools.partial(kernel, n_slab, n_sub),
         out_shape=(
             jax.ShapeDtypeStruct((NB_DEV, block), f32),
             jax.ShapeDtypeStruct((tiles, rows), f32),
         ),
-        in_specs=[pl.BlockSpec(memory_space=pl.ANY), scalars, scalars, whole],
+        in_specs=[pl.BlockSpec(memory_space=pl.ANY)] * 4,
         out_specs=(whole, whole),
         scratch_shapes=[
             vmem(values.shape, f32),
@@ -387,6 +400,10 @@
             vmem((window, LANES), f32),
             vmem((ITERS, n, 1, LANES), f32),
             vmem((ITERS, n, 2, LANES), f32),
+            pltpu.SMEM((tiles, coupled), jnp.int32),
+            pltpu.SMEM((1, 1), jnp.int32),
+            vmem((tiles, rows), f32),
+            dma((3,)),
             dma((tiles,)),
             dma((slots,)),
             dma((slots,)),

time: 66.9 us -> 61.2 us (0.915)
  Pallas kernels: 62.6 us -> 56.9 us
    pallas_call x1, Pallas kernels: 62.6 us -> 56.9 us  [per_device(): pl.pallas_call(functools.partial(kernel, n_slab, n_sub), out_shape=(jax.S...]
where the time goes in v2:
time: 61.2 us; the launch traced here: 60.9 us
  Pallas kernels  56.9 us (93%)
  local copies, waits for them, and re-layouts  2.67 us (4%)
  between operations  1.29 us (2%)
    pallas_call x1, Pallas kernels, per_device(): pl.pallas_call(functools.partial(kernel, n_slab, n_sub), out_shape=(jax.S...  56.9 us
    unnamed x5, local copies, waits for them, and re-layouts  2.67 us

profile of v2, /device:TPU:0, one launch (start us, length us, event | category | flops | bytes accessed | tf_op | source)
XLA Modules:
  0.0 60.9 jit_solution(17592848961844889520)
XLA Ops:
  1.3 0.8 %copy.6.ids_hbm = s32[24,2]{1,0:T(8,128)S(1)} copy(s32[24,2]{0,1:T(2,128)} %param.5) | data formatting | bytes 384 | tf_op args[1]
  2.0 0.0 copy-start
  2.0 0.7 %copy-done = f32[24,128]{1,0:T(8,128)S(1)} copy-done((f32[24,128]{1,0:T(8,128)S(1)}, f32[24,128]{1,0:T(8,128)}, u32[]{:S(2)}) %copy-start) | copy-done | bytes 12312
  2.7 56.9 %shard_map.59 = (f32[12,256]{1,0:T(8,128)S(1)}, f32[24,128]{1,0:T(8,128)S(1)}) custom-call(f32[24,2,128,256]{3,2,1,0:T(8,128)} %values_hbm.1, s32[24,2]{1,0:T(8,128)S(1)} %copy.6.ids_hbm, s32[1,1]{1,0:T(1,128)S(6)} %copy.9.counts_hbm, f32[24,128]{1,0:T(8,128)S(1)} %copy-done), custom_call_target="tpu_custom_call" | custom-call | tf_op jit(solution)/shard_map/pallas_call | solution.py:376
  59.7 0.6 copy.10
  60.3 0.6 copy.11
Async XLA Ops:
  2.0 0.7 %copy-start = (f32[24,128]{1,0:T(8,128)S(1)}, f32[24,128]{1,0:T(8,128)}, u32[]{:S(2)}) copy-start(f32[24,128]{1,0:T(8,128)} %right_hbm.1) | copy-start | bytes 36868

commit v3 on v2

--- a/solution.py
+++ b/solution.py
@@ -40,8 +40,7 @@
     part_in,
     field_out,
     field_in,
-    scaled_win,
-    direction_win,
+    field_win,
     scal1,
     scal2,
     ids_smem,
@@ -272,26 +271,21 @@
     field_out[0] = scaled
     rho_part = total(normal_res * scaled)
     scal2[0, me] = jnp.broadcast_to(rho_part, (2, LANES))
+    start_all(functools.partial(field_copy, 0), False)
     scal_start(scal2, scal2_send, scal2_recv, 0)
-    start_all(functools.partial(field_copy, 0), False)
     field_in[0, own_rel, sub] = scaled
     wait_recv_all(functools.partial(field_copy, 0), False)
-    scaled_win[...] = field_in[0].reshape(window, LANES)
-    direction_win[...] = scaled_win[...]
-    scal_all(scal2, scal2_send, scal2_recv, 0).wait_recv()
-    rho_now = jnp.sum(scal2[0], axis=0)[0:1]
-
     answer = jnp.zeros((held, LANES), f32)
-    own_rows = pl.ds(pl.multiple_of((n_sub + sub) * held, 8), held)
     for it in range(ITERS):
         last = it == ITERS - 1
-
-        def tile_pass(t, norm):
+        field_win[...] = field_in[it].reshape(window, LANES)
+
+        def tile_pass(t, carry):
             alive = live(t)
             m = None
             for k in range(coupled):
                 for h in range(halves):
-                    picked = direction_win[pl.ds(wid[t, k] + h * NB_DEV, 1), :] * alive
+                    picked = field_win[pl.ds(wid[t, k] + h * NB_DEV, 1), :] * alive
                     product = values[t, k, :, half(h)] * picked
                     m = product if m is None else m + product
             image = jnp.broadcast_to(jnp.sum(m, axis=1, keepdims=True), (rows, LANES))
@@ -302,10 +296,9 @@
                         terms[term_row(k, h, t), :] = jnp.sum(
                             values[t, k, :, half(h)] * image, axis=0, keepdims=True
                         )
-            return norm + jnp.sum(image * image, axis=0, keepdims=True)
-
-        norm = lax.fori_loop(0, tiles, tile_pass, jnp.zeros((1, LANES), f32), unroll=2)
-        scal1[it, me] = norm
+            return carry
+
+        lax.fori_loop(0, tiles, tile_pass, 0, unroll=8)
         if not last:
             part_out[it] = scatter((terms,))[0]
             out_copy = functools.partial(
@@ -313,36 +306,59 @@
             )
             part_in[it, own_slot] = part_out[it, own_rel, sub]
             start_all(out_copy, True)
-        scal_start(scal1, scal1_send, scal1_recv, it)
-
-        @pl.loop(0, tiles)
+
+        @pl.loop(0, tiles, unroll=4)
         def _(t):
             image_rows[pl.ds(t, 1), :] = jnp.sum(image_cols[t] * eye, axis=0, keepdims=True)
 
+        field_own = field_in[it, 1, sub]
+        if it == 0:
+            scal_all(scal2, scal2_send, scal2_recv, 0).wait_recv()
+            rho_now = jnp.sum(scal2[0], axis=0)[0:1]
+            scaled_own = field_own
+            direction = field_own
+            scaled_image = image_rows[...]
+            image = scaled_image
+        else:
+            scal_all(scal1, scal1_send, scal1_recv, it - 1).wait_recv()
+            step_size = rho_now / jnp.sum(scal1[it - 1], axis=0)
+            answer = answer + step_size * direction
+            residual_ref[...] = residual_ref[...] - step_size * image
+            scaled = scaled - step_size * back_scaled
+            scal_all(scal2, scal2_send, scal2_recv, it).wait_recv()
+            both = jnp.sum(scal2[it], axis=0)
+            rho_next = rho_now - 2.0 * step_size * both[0:1] + step_size * step_size * both[1:2]
+            beta = rho_next / rho_now
+            rho_now = rho_next
+            scaled_own = scaled_own - step_size * field_own
+            direction = scaled_own + beta * direction
+            scaled_image = scaled_image - step_size * image_rows[...]
+            image = scaled_image + beta * image
+        scal1[it, me] = jnp.broadcast_to(total(image * image), (1, LANES))
+        scal_start(scal1, scal1_send, scal1_recv, it)
+
         if not last:
             wait_recv_all(out_copy, True)
-            back = jnp.sum(part_in[it], axis=0)
+            spread = jnp.sum(part_in[it], axis=0)
+            if it == 0:
+                scaled_back = spread
+                back = spread
+            else:
+                scaled_back = scaled_back - step_size * spread
+                back = scaled_back + beta * back
             back_scaled = jacobi * back
             field_out[it + 1] = back_scaled
+            start_all(functools.partial(field_copy, it + 1), False)
             scal2[it + 1, me, 0:1] = jnp.broadcast_to(total(scaled * back), (1, LANES))
             scal2[it + 1, me, 1:2] = jnp.broadcast_to(total(back * back_scaled), (1, LANES))
             scal_start(scal2, scal2_send, scal2_recv, it + 1)
-            start_all(functools.partial(field_copy, it + 1), False)
             field_in[it + 1, own_rel, sub] = back_scaled
-        scal_all(scal1, scal1_send, scal1_recv, it).wait_recv()
-        step_size = rho_now / jnp.sum(scal1[it], axis=0)
-        answer = answer + step_size * direction_win[own_rows, :]
-        residual_ref[...] = residual_ref[...] - step_size * image_rows[...]
-        if not last:
-            scaled = scaled - step_size * back_scaled
             wait_recv_all(functools.partial(field_copy, it + 1), False)
-            scaled_win[...] = scaled_win[...] - step_size * field_in[it + 1].reshape(window, LANES)
-            scal_all(scal2, scal2_send, scal2_recv, it + 1).wait_recv()
-            both = jnp.sum(scal2[it + 1], axis=0)
-            rho_next = rho_now - 2.0 * step_size * both[0:1] + step_size * step_size * both[1:2]
-            direction_win[...] = scaled_win[...] + (rho_next / rho_now) * direction_win[...]
-            rho_now = rho_next
-
+
+    scal_all(scal1, scal1_send, scal1_recv, ITERS - 1).wait_recv()
+    step_size = rho_now / jnp.sum(scal1[ITERS - 1], axis=0)
+    answer = answer + step_size * direction
+    residual_ref[...] = residual_ref[...] - step_size * image
     for h in range(halves):
         solution_ref[:, half(h)] = answer[h * NB_DEV : (h + 1) * NB_DEV]
 
@@ -397,7 +413,6 @@
             vmem((ITERS, held, LANES), f32),
             vmem((ITERS, 3, n_sub, held, LANES), f32),
             vmem((window, LANES), f32),
-            vmem((window, LANES), f32),
             vmem((ITERS, n, 1, LANES), f32),
             vmem((ITERS, n, 2, LANES), f32),
             pltpu.SMEM((tiles, coupled), jnp.int32),

time: 61.2 us -> 55.7 us (0.910)
  Pallas kernels: 56.9 us -> 51.5 us
    pallas_call x1, Pallas kernels: 56.9 us -> 51.5 us  [per_device(): pl.pallas_call(functools.partial(kernel, n_slab, n_sub), out_shape=(jax.S...]
where the time goes in v3:
time: 55.7 us; the launch traced here: 55.4 us
  Pallas kernels  51.5 us (92%)
  local copies, waits for them, and re-layouts  2.67 us (5%)
  between operations  1.29 us (2%)
    pallas_call x1, Pallas kernels, per_device(): pl.pallas_call(functools.partial(kernel, n_slab, n_sub), out_shape=(jax.S...  51.5 us
    unnamed x5, local copies, waits for them, and re-layouts  2.67 us

profile of v3, /device:TPU:0, one launch (start us, length us, event | category | flops | bytes accessed | tf_op | source)
XLA Modules:
  0.0 55.4 jit_solution(1248452761134390583)
XLA Ops:
  1.3 0.8 %copy.6.ids_hbm = s32[24,2]{1,0:T(8,128)S(1)} copy(s32[24,2]{0,1:T(2,128)} %param.5) | data formatting | bytes 384 | tf_op args[1]
  2.0 0.0 copy-start
  2.0 0.7 %copy-done = f32[24,128]{1,0:T(8,128)S(1)} copy-done((f32[24,128]{1,0:T(8,128)S(1)}, f32[24,128]{1,0:T(8,128)}, u32[]{:S(2)}) %copy-start) | copy-done | bytes 12312
  2.7 51.5 %shard_map.59 = (f32[12,256]{1,0:T(8,128)S(1)}, f32[24,128]{1,0:T(8,128)S(1)}) custom-call(f32[24,2,128,256]{3,2,1,0:T(8,128)} %values_hbm.1, s32[24,2]{1,0:T(8,128)S(1)} %copy.6.ids_hbm, s32[1,1]{1,0:T(1,128)S(6)} %copy.9.counts_hbm, f32[24,128]{1,0:T(8,128)S(1)} %copy-done), custom_call_target="tpu_custom_call" | custom-call | tf_op jit(solution)/shard_map/pallas_call | solution.py:392
  54.2 0.6 %copy.10 = f32[12,256]{1,0:T(8,128)} copy(f32[12,256]{1,0:T(8,128)S(1)} %get-tuple-element.4) | data formatting | bytes 24576
  54.8 0.6 %copy.11 = f32[24,128]{1,0:T(8,128)} copy(f32[24,128]{1,0:T(8,128)S(1)} %get-tuple-element.5) | data formatting | bytes 24576
Async XLA Ops:
  2.0 0.7 %copy-start = (f32[24,128]{1,0:T(8,128)S(1)}, f32[24,128]{1,0:T(8,128)}, u32[]{:S(2)}) copy-start(f32[24,128]{1,0:T(8,128)} %right_hbm.1) | copy-start | bytes 36868

commit v4 on v3

--- a/solution.py
+++ b/solution.py
@@ -167,7 +167,7 @@
 
     def each(act, scatters):
         for ds in (1, -1, 0):
-            for step in range(n_sub):
+            for step in (*range(1, n_sub), 0):
                 if scatters:
                     exists, far = inside(slab + ds), keeper(slab + ds)
                 else:

time: 55.7 us -> 54.9 us (0.986)
  Pallas kernels: 51.5 us -> 50.7 us
    pallas_call x1, Pallas kernels: 51.5 us -> 50.7 us  [per_device(): pl.pallas_call(functools.partial(kernel, n_slab, n_sub), out_shape=(jax.S...]
where the time goes in v4:
time: 54.9 us; the launch traced here: 54.6 us
  Pallas kernels  50.7 us (92%)
  local copies, waits for them, and re-layouts  2.67 us (5%)
  between operations  1.29 us (2%)
    pallas_call x1, Pallas kernels, per_device(): pl.pallas_call(functools.partial(kernel, n_slab, n_sub), out_shape=(jax.S...  50.7 us
    unnamed x5, local copies, waits for them, and re-layouts  2.67 us

profile of v4, /device:TPU:0, one launch (start us, length us, event | category | flops | bytes accessed | tf_op | source)
XLA Modules:
  0.0 54.6 jit_solution(15587008768296394147)
XLA Ops:
  1.3 0.8 %copy.6.ids_hbm = s32[24,2]{1,0:T(8,128)S(1)} copy(s32[24,2]{0,1:T(2,128)} %param.5) | data formatting | bytes 384 | tf_op args[1]
  2.0 0.0 copy-start
  2.0 0.7 %copy-done = f32[24,128]{1,0:T(8,128)S(1)} copy-done((f32[24,128]{1,0:T(8,128)S(1)}, f32[24,128]{1,0:T(8,128)}, u32[]{:S(2)}) %copy-start) | copy-done | bytes 12312
  2.7 50.7 %shard_map.59 = (f32[12,256]{1,0:T(8,128)S(1)}, f32[24,128]{1,0:T(8,128)S(1)}) custom-call(f32[24,2,128,256]{3,2,1,0:T(8,128)} %values_hbm.1, s32[24,2]{1,0:T(8,128)S(1)} %copy.6.ids_hbm, s32[1,1]{1,0:T(1,128)S(6)} %copy.9.counts_hbm, f32[24,128]{1,0:T(8,128)S(1)} %copy-done), custom_call_target="tpu_custom_call" | custom-call | tf_op jit(solution)/shard_map/pallas_call | solution.py:392
  53.4 0.6 %copy.10 = f32[12,256]{1,0:T(8,128)} copy(f32[12,256]{1,0:T(8,128)S(1)} %get-tuple-element.4) | data formatting | bytes 24576
  54.0 0.6 %copy.11 = f32[24,128]{1,0:T(8,128)} copy(f32[24,128]{1,0:T(8,128)S(1)} %get-tuple-element.5) | data formatting | bytes 24576
Async XLA Ops:
  2.0 0.7 %copy-start = (f32[24,128]{1,0:T(8,128)S(1)}, f32[24,128]{1,0:T(8,128)}, u32[]{:S(2)}) copy-start(f32[24,128]{1,0:T(8,128)} %right_hbm.1) | copy-start | bytes 36868
